TPU v7x, 32 devices: a whole 2x2x4 slice. The times are simulated.
32 devices in a mesh: grp: 8 (over y, x, core), mem: 4 (over z).
Axes of the slice: x: 2, y: 2, z: 4, core: 2. Of those that a mesh axis runs over, the one named last changes fastest.
Arguments:
- dyn_state: float32 [2, 58, 32, 128], P(None, None, 'grp', 'mem'), may hold values from -6 to 6
- wind_speed: float32 [58, 32, 128], P(None, 'grp', 'mem'), may hold values from -4 to 4
- mass_weight: float32 [32, 128], P('grp', 'mem'), may hold values from 0.5 to 2
- crm_state: float32 [1024, 58, 128], P(('grp', 'mem')), may hold values from -6 to 6
- batch_map: int32 [1024], P(('grp', 'mem')), may hold values from 0 to 127, as said below
- sub_steps: int32 [1024], P(('grp', 'mem')), may hold values from 1 to 2
- migrate_to: int32 [1024], P(('grp', 'mem')), may hold values from 0 to 1023, as said below
Outputs:
- dyn_next: float32 [2, 58, 32, 128], P(None, None, 'grp', 'mem')
- phys_tend: float32 [2, 58, 1024], P(None, None, ('grp', 'mem'))
- crm_next: float32 [1024, 58, 128], P(('grp', 'mem'))
Inputs may be any that keep to these rules, and one draw needn't show every extreme that they name: `batch_map`: within each aligned block of 128 slots (one group), the entries are a permutation of 0 to 127. `migrate_to`: A permutation of all slots. Every slot goes to a device with the same mem index. Exactly 4 of one device's slots leave its group, at most one of them to any one other device; the rest move within the device.
All inputs are finite; a program needn't handle non-finite values.
Results may differ from a plain program's by a relative error of at most 0.0003.
Values sent between devices are 32-bit elements; how exact they have to be, the bound alone decides.
A program may use at most 64 MiB of HBM per device.

v0:
```python
import jax
import jax.numpy as jnp
import numpy as np
from jax import lax
from jax.sharding import PartitionSpec as P

NSUB = 2


def extended(array, sides, width):
    for axis, dim in sides:
        peers, length = (lax.axis_size(axis), array.shape[dim])
        up = [(i, (i + 1) % peers) for i in range(peers)]
        down = [(j, i) for i, j in up]
        last = lax.slice_in_dim(array, length - width, length, axis=dim)
        first = lax.slice_in_dim(array, 0, width, axis=dim)
        before = lax.ppermute(last, axis, up)
        after = lax.ppermute(first, axis, down)
        array = jnp.concatenate([before, array, after], axis=dim)
    return array


def derivative_table():
    nodes = np.array([-1.0, -1.0 / np.sqrt(5.0), 1.0 / np.sqrt(5.0), 1.0])
    table = np.zeros((4, 4))
    for target_node in range(4):
        for source_node in range(4):
            if target_node == source_node:
                table[target_node, source_node] = sum(
                    (
                        1.0 / (nodes[source_node] - nodes[other_node])
                        for other_node in range(4)
                        if other_node != source_node
                    )
                )
            else:
                numerator = 1.0
                for other_node in range(4):
                    if other_node != source_node and other_node != target_node:
                        numerator = numerator * (nodes[target_node] - nodes[other_node])
                denominator = 1.0
                for other_node in range(4):
                    if other_node != source_node:
                        denominator = denominator * (nodes[source_node] - nodes[other_node])
                table[target_node, source_node] = numerator / denominator
    return table.astype(np.float32)


def element_derivative(field):
    shape_in = field.shape
    blocks = field.reshape(shape_in[:-1] + (shape_in[-1] // 4, 4))
    table = jnp.asarray(derivative_table())
    result = jnp.einsum("...ej,ij->...ei", blocks, table, precision=lax.Precision.HIGHEST)
    return result.reshape(shape_in)


def assemble_padded(values, axis):
    length = values.shape[axis] - 2
    shape_b = [1] * values.ndim
    shape_b[axis] = length
    position = jnp.arange(length, dtype=jnp.int32)
    opening = (position % 4 == 0).reshape(shape_b)
    closing = (position % 4 == 3).reshape(shape_b)
    center = lax.slice_in_dim(values, 1, length + 1, axis=axis)
    before = lax.slice_in_dim(values, 0, length, axis=axis)
    after = lax.slice_in_dim(values, 2, length + 2, axis=axis)
    return center + jnp.where(opening, before, 0.0) + jnp.where(closing, after, 0.0)


def second_levels(values):
    upper = jnp.concatenate([values[:, 1:], values[:, -1:]], 1)
    lower = jnp.concatenate([values[:, :1], values[:, :-1]], 1)
    return upper + lower - 2.0 * values


def crm_run(state, forcing, steps):
    width = state.shape[-1] // 2
    lanes = jnp.arange(2 * width, dtype=jnp.int32)
    heat_lane = (lanes < width)[None, None, :]
    first_lane = (lanes % width == 0)[None, None, :]
    last_lane = (lanes % width == width - 1)[None, None, :]
    forcing_lanes = jnp.where(heat_lane, forcing[0].T[:, :, None], forcing[1].T[:, :, None])
    condense_sign = jnp.where(heat_lane, 0.5, -1.0)
    current = state
    for substep in range(NSUB):
        other = jnp.roll(current, width, -1)
        gap = jnp.where(heat_lane, other - current, current - other)
        condense = 0.1 * jax.nn.softplus(gap)
        left = jnp.where(first_lane, jnp.roll(current, 1 - width, -1), jnp.roll(current, 1, -1))
        right = jnp.where(last_lane, jnp.roll(current, width - 1, -1), jnp.roll(current, -1, -1))
        columns_term = left + right - 2.0 * current
        updated = (
            current
            + 0.25 * forcing_lanes
            + 0.15 * columns_term
            + 0.1 * second_levels(current)
            + condense_sign * condense
        )
        active = (steps > substep)[:, None, None]
        current = jnp.where(active, updated, current)
    change = current - state
    halves = change.reshape(change.shape[0], change.shape[1], 2, width).mean(-1)
    tendency = halves.transpose(2, 1, 0)
    return (current, tendency)


def relocate(state, side, migrate_to):
    slots = migrate_to.shape[0]
    group_size = lax.axis_size("grp")
    member_size = lax.axis_size("mem")
    dest_group = migrate_to // (member_size * slots)
    dest_slot = migrate_to % slots
    own_group = lax.axis_index("grp")
    staying = dest_group == own_group
    kept_target = jnp.where(staying, dest_slot, slots)
    retained_state = jnp.zeros_like(state).at[kept_target].set(state, mode="drop")
    kept_side = jnp.zeros_like(side).at[kept_target].set(side, mode="drop")
    outgoing = jnp.where(staying, group_size, dest_group)
    sender = (
        jnp.zeros((group_size,), jnp.int32)
        .at[outgoing]
        .set(jnp.arange(slots, dtype=jnp.int32), mode="drop")
    )
    filled_rows = jnp.zeros((group_size,), jnp.float32).at[outgoing].set(1.0, mode="drop")
    marker = filled_rows * (dest_slot[sender].astype(jnp.float32) + 1.0)
    bucket_state = state[sender] * filled_rows[:, None, None]
    holding_bucket_side = jnp.concatenate([side[sender] * filled_rows[:, None], marker[:, None]], 1)
    arrived_state, arrived_side = (
        lax.all_to_all(bucket_state, "grp", split_axis=0, concat_axis=0, tiled=True),
        lax.all_to_all(holding_bucket_side, "grp", split_axis=0, concat_axis=0, tiled=True),
    )
    target = arrived_side[:, -1].astype(jnp.int32) - 1
    target = jnp.where(target < 0, slots, target)
    new_state = retained_state.at[target].set(arrived_state, mode="drop")
    new_side = kept_side.at[target].set(arrived_side[:, :-1], mode="drop")
    return (new_state, new_side)


def on_device(dyn_state, wind_speed, mass_weight, crm_state, batch_map, sub_steps, migrate_to):
    levels = dyn_state.shape[1]
    rows_local = dyn_state.shape[2]
    points_local = dyn_state.shape[3]
    slots = crm_state.shape[0]
    advection = -wind_speed[None] * element_derivative(dyn_state)
    stacked = jnp.concatenate(
        [
            (mass_weight[None, None] * advection).reshape(2 * levels, rows_local, points_local),
            mass_weight[None],
        ],
        0,
    )
    padded = extended(stacked, (("grp", 1), ("mem", 2)), 1)
    swept = assemble_padded(assemble_padded(padded, 2), 1)
    numerator = swept[: 2 * levels].reshape(2, levels, rows_local, points_local)
    assembled = numerator / swept[2 * levels]
    dyn_next = dyn_state + 0.2 * assembled
    forcing = (
        assembled.reshape(2, levels, rows_local // 2, 2, points_local // 2, 2)
        .mean((3, 5))
        .reshape(2, levels, slots)
    )
    partition_piece = lax.all_gather(forcing, "mem", axis=2, tiled=True)
    length = partition_piece.shape[2]
    column_picker = (batch_map[None, :] == jnp.arange(length, dtype=jnp.int32)[:, None]).astype(
        jnp.float32
    )
    forcing_position = jnp.einsum(
        "zoy,yd->zod", partition_piece, column_picker, precision=lax.Precision.HIGHEST
    )
    stepped, tendency_slot = crm_run(crm_state, forcing_position, sub_steps)
    crm_next, unused_side = relocate(stepped, jnp.zeros((slots, 0), jnp.float32), migrate_to)
    flat_tendency = tendency_slot.reshape(2 * levels, slots)
    column_picker = (
        batch_map[None, :] == jnp.arange(slots * lax.axis_size("mem"), dtype=jnp.int32)[:, None]
    ).astype(jnp.float32)
    gathered_rows = lax.psum_scatter(
        jnp.einsum("cs,ks->ck", column_picker, flat_tendency, precision=lax.Precision.HIGHEST),
        "mem",
        scatter_dimension=0,
        tiled=True,
    )
    phys_tend = gathered_rows.reshape(slots, 2, levels).transpose(1, 2, 0)
    return (dyn_next, phys_tend, crm_next)


def solution(mesh):
    placed = (
        P(None, None, "grp", "mem"),
        P(None, "grp", "mem"),
        P("grp", "mem"),
        P(("grp", "mem"), None, None),
        P(("grp", "mem")),
        P(("grp", "mem")),
        P(("grp", "mem")),
    )
    return jax.shard_map(
        on_device,
        mesh=mesh,
        in_specs=placed,
        out_specs=(
            P(None, None, "grp", "mem"),
            P(None, None, ("grp", "mem")),
            P(("grp", "mem"), None, None),
        ),
        check_vma=False,
    )
```

profile of v0, /device:TPU:0, one launch (start us, length us, event | category | flops | bytes accessed | tf_op | source)
XLA Modules:
  0.0 119.6 jit_solution(2821653146365642949)
XLA Ops:
  7.2 1.4 %convolution_bitcast_fusion = f32[2,58,4,8,4]{1,4,3,2,0:T(4,128)S(1)} fusion(f32[4,4,1,1,1]{1,0,4,3,2:T(4,128)} %constant.132, f32[2,58,4,8,4]{1,4,3,2,0:T(4,128)} %bitcast.49), kind=kOutput, calls=%fused_computation.8 | convolution fusion | flops 712704 | bytes 118848 | tf_op jit(solution)/shard_map/...ej,ij->...ei/dot_general | solution.py:53
  8.8 0.8 neg.11
  9.8 0.8 copy.129
  10.6 0.8 multiply_multiply_fusion
  11.4 0.5 collective-permute-start
  11.9 2.9 %collective-permute-start.1 = (f32[117,1,32]{0,2,1:T(8,128)S(1)}, f32[117,1,32]{0,2,1:T(8,128)S(1)}, u32[]{:S(2)}, u32[]{:S(2)}) collective-permute-start(f32[117,1,32]{0,2,1:T(8,128)S(1)} %get-tuple-element.53), channel_id=1, source_target_pairs={{4,0},{8,4},{12,8},{16,12},{20,16},{24,20},{28,24},{0,28},{5,1},{9... | collective-permute-start | bytes 44936 | tf_op jit(solution)/shard_map/ppermute | solution.py:18
  14.9 0.7 compare_select_fusion.5
  15.5 0.7 compare_select_fusion.6
  16.2 0.7 scatter_custom_fusion.2
  16.9 0.7 scatter_custom_fusion.1
  17.6 0.6 gather_fusion
  18.2 0.7 copy.138
  18.9 3.5 %all-to-all-start = ((f32[8,1,1]{2,1,0:T(1,128)}), f32[8,1,1]{2,1,0:T(1,128)S(1)}, u32[]{:S(2)}, u32[]{:S(2)}) async-start(f32[8,1,1]{2,1,0:T(1,128)} %copy.138), calls=%async_computation.1 | async-start | bytes 8192 | tf_op jit(solution)/shard_map/all_to_all | solution.py:130
  22.5 1.3 %fusion.46 = (f32[32,58,64]{2,0,1:T(8,128)S(1)}, f32[32,58,64]{2,0,1:T(8,128)}) fusion(f32[32,58,128]{2,0,1:T(8,128)S(1)} %copy-done), kind=kLoop, calls=%fused_computation.115 | loop fusion | bytes 1900544 | tf_op jit(solution)/shard_map/jit(_roll_static)/slice | solution.py:86
  23.7 1.6 %fusion.49 = (f32[32,58,127]{2,0,1:T(8,128)}, f32[32,58,127]{2,0,1:T(8,128)}) fusion(f32[32,58,128]{2,0,1:T(8,128)S(1)} %copy-done), kind=kLoop, calls=%fused_computation.118 | loop fusion | bytes 3771392 | tf_op jit(solution)/shard_map/jit(_roll_static)/slice | solution.py:90
  25.3 1.6 %fusion.50 = (f32[32,58,1]{2,0,1:T(8,128)}, f32[32,58,1]{2,0,1:T(8,128)}) fusion(f32[32,58,128]{2,0,1:T(8,128)S(1)} %copy-done), kind=kLoop, calls=%fused_computation.119 | loop fusion | bytes 29696 | tf_op jit(solution)/shard_map/jit(_roll_static)/slice | solution.py:90
  27.0 1.6 %fusion.51 = (f32[32,58,63]{2,0,1:T(8,128)}, f32[32,58,63]{2,0,1:T(8,128)}) fusion(f32[32,58,128]{2,0,1:T(8,128)S(1)} %copy-done), kind=kLoop, calls=%fused_computation.120 | loop fusion | bytes 1870848 | tf_op jit(solution)/shard_map/jit(_roll_static)/slice | solution.py:90
  28.6 1.6 %fusion.52 = (f32[32,58,65]{2,0,1:T(8,128)}, f32[32,58,65]{2,0,1:T(8,128)}) fusion(f32[32,58,128]{2,0,1:T(8,128)S(1)} %copy-done), kind=kLoop, calls=%fused_computation.121 | loop fusion | bytes 1930240 | tf_op jit(solution)/shard_map/jit(_roll_static)/slice | solution.py:90
  30.2 1.5 %fusion.48 = (f32[32,57,128]{2,0,1:T(8,128)}, f32[32,57,128]{2,0,1:T(8,128)}) fusion(f32[32,58,128]{2,0,1:T(8,128)S(1)} %copy-done), kind=kLoop, calls=%fused_computation.117 | loop fusion | bytes 3735552 | tf_op jit(solution)/shard_map/slice | solution.py:72
  31.8 0.2 add_reduce_fusion
  32.1 2.1 %collective-permute-start.2 = (f32[117,6,1]{0,2,1:T(1,128)S(1)}, f32[117,6,1]{0,2,1:T(1,128)S(1)}, u32[]{:S(2)}, u32[]{:S(2)}) collective-permute-start(f32[117,6,1]{0,2,1:T(1,128)S(1)} %get-tuple-element.54), channel_id=1, source_target_pairs={{0,1},{1,2},{2,3},{3,0},{4,5},{5,6},{6,7},{7,4},{8,9},{9,10},{10,1... | collective-permute-start | bytes 8432 | tf_op jit(solution)/shard_map/ppermute | solution.py:17
  34.3 2.1 %collective-permute-start.3 = (f32[117,6,1]{0,2,1:T(1,128)S(1)}, f32[117,6,1]{0,2,1:T(1,128)S(1)}, u32[]{:S(2)}, u32[]{:S(2)}) collective-permute-start(f32[117,6,1]{0,2,1:T(1,128)S(1)} %get-tuple-element.55), channel_id=1, source_target_pairs={{1,0},{2,1},{3,2},{0,3},{5,4},{6,5},{7,6},{4,7},{9,8},{10,9},{11,1... | collective-permute-start | bytes 8432 | tf_op jit(solution)/shard_map/ppermute | solution.py:18
  36.4 1.5 %collective-permute-done.2 = f32[117,6,1]{0,2,1:T(1,128)S(1)} collective-permute-done((f32[117,6,1]{0,2,1:T(1,128)S(1)}, f32[117,6,1]{0,2,1:T(1,128)S(1)}, u32[]{:S(2)}, u32[]{:S(2)}) %collective-permute-start.2) | collective-permute-done | bytes 2840 | tf_op jit(solution)/shard_map/ppermute | solution.py:17
  38.8 13.6 %all_gather.3 = f32[2,58,128]{1,2,0:T(8,128)S(1)} all-gather(f32[2,58,32]{1,2,0:T(8,128)S(1)} %bitcast.50), channel_id=1, replica_groups=mesh['grp'=8,'mem'=4] {'mem'}, dimensions={2}, use_global_device_ids=true | all-gather | bytes 74240 | tf_op jit(solution)/shard_map/all_gather | solution.py:162
  52.8 5.1 %fusion.2 = f32[32,58,128]{2,0,1:T(8,128)S(1)} fusion(f32[32,58,128]{2,0,1:T(8,128)S(1)} %copy-done, f32[32,58,63]{2,0,1:T(8,128)} %get-tuple-element.49, f32[32,58,65]{2,0,1:T(8,128)} %get-tuple-element.51, f32[32,58,127]{2,0,1:T(8,128)} %get-tuple-element.45, f32[32,58,1]{2,0,1:T(8,128)} %get-tuple-element.47, f32[32,58,65]{2,0,1:T(8,128)} %get-tuple-element.50, ...), kind=kLoop, calls=%fused_computation.11 | loop fusion | flops 7839744 | bytes 8568224 | tf_op jit(solution)/shard_map/jit(_where)/select_n | solution.py:100
  57.9 1.3 %fusion.39 = (f32[32,58,65]{2,0,1:T(8,128)S(1)}, f32[32,58,65]{2,0,1:T(8,128)}) fusion(f32[32,58,128]{2,0,1:T(8,128)S(1)} %fusion.2), kind=kLoop, calls=%fused_computation.108 | loop fusion | bytes 1930240 | tf_op jit(solution)/shard_map/jit(_roll_static)/slice | solution.py:89
  59.2 1.7 %fusion.40 = (f32[32,58,63]{2,0,1:T(8,128)}, f32[32,58,63]{2,0,1:T(8,128)}) fusion(f32[32,58,128]{2,0,1:T(8,128)S(1)} %fusion.2), kind=kLoop, calls=%fused_computation.109 | loop fusion | bytes 1870848 | tf_op jit(solution)/shard_map/jit(_roll_static)/slice | solution.py:89
  60.9 1.6 %fusion.41 = (f32[32,58,1]{2,0,1:T(8,128)}, f32[32,58,1]{2,0,1:T(8,128)}) fusion(f32[32,58,128]{2,0,1:T(8,128)S(1)} %fusion.2), kind=kLoop, calls=%fused_computation.110 | loop fusion | bytes 29696 | tf_op jit(solution)/shard_map/jit(_roll_static)/slice | solution.py:89
  62.4 1.6 %fusion.42 = (f32[32,58,127]{2,0,1:T(8,128)}, f32[32,58,127]{2,0,1:T(8,128)}) fusion(f32[32,58,128]{2,0,1:T(8,128)S(1)} %fusion.2), kind=kLoop, calls=%fused_computation.111 | loop fusion | bytes 3771392 | tf_op jit(solution)/shard_map/jit(_roll_static)/slice | solution.py:89
  64.0 1.6 %fusion.45 = (f32[32,58,64]{2,0,1:T(8,128)}, f32[32,58,64]{2,0,1:T(8,128)}) fusion(f32[32,58,128]{2,0,1:T(8,128)S(1)} %fusion.2), kind=kLoop, calls=%fused_computation.114 | loop fusion | bytes 1900544 | tf_op jit(solution)/shard_map/jit(_roll_static)/slice | solution.py:86
  65.6 1.6 %fusion.43 = (f32[32,57,128]{2,0,1:T(8,128)}, f32[32,57,128]{2,0,1:T(8,128)}) fusion(f32[32,58,128]{2,0,1:T(8,128)S(1)} %fusion.2), kind=kLoop, calls=%fused_computation.112 | loop fusion | bytes 3735552 | tf_op jit(solution)/shard_map/slice | solution.py:71
  67.3 6.1 %fusion.37 = (f32[32,58,128]{2,0,1:T(8,128)}, f32[32,58,128]{2,0,1:T(8,128)S(1)}) fusion(f32[32,58,128]{2,0,1:T(8,128)S(1)} %copy-done, f32[32,58,128]{2,0,1:T(8,128)S(1)} %fusion.2, f32[128]{0:T(128)S(1)} %select_multiply_fusion.1, f32[32,58,64]{2,0,1:T(8,128)} %get-tuple-element.37, f32[32,58,64]{2,0,1:T(8,128)} %get-tuple-element.36, ...), kind=kLoop, calls=%fused_computation.107 | loop fusion | flops 8077312 | bytes 10468768 | tf_op jit(solution)/shard_map/sub | solution.py:101
  73.4 0.6 copy.137
  74.0 0.6 gather_fusion.1
  74.5 0.8 broadcast_multiply_fusion
  75.3 4.1 %all-to-all-start.1 = ((f32[8,58,128]{2,1,0:T(8,128)}), f32[8,58,128]{2,1,0:T(8,128)S(1)}, u32[]{:S(2)}, u32[]{:S(2)}) async-start(f32[8,58,128]{2,1,0:T(8,128)} %broadcast_multiply_fusion), calls=%async_computation.2 | async-start | bytes 524288 | tf_op jit(solution)/shard_map/all_to_all | solution.py:129
  79.6 2.4 %reshape.135 = f32[32,58,2,64]{3,2,0,1:T(2,128)S(1)} reshape(f32[32,58,128]{2,0,1:T(8,128)} %get-tuple-element.22) | data formatting | bytes 1900544 | tf_op jit(solution)/shard_map/reshape | solution.py:102
  82.0 3.0 %reduce_sum.19 = f32[32,58,2]{2,0,1:T(8,128)} reduce(f32[32,58,2,64]{3,2,0,1:T(2,128)S(1)} %reshape.135, f32[]{:T(128)} %constant.107.clone.1), dimensions={3}, to_apply=%region_1.2 | reduce | flops 233856 | bytes 965124 | tf_op jit(solution)/shard_map/reduce_sum | solution.py:102
  85.0 1.3 %multiply_bitcast_fusion = f32[2,58,32]{0,2,1:T(8,128)S(1)} fusion(f32[32,58,2]{2,0,1:T(8,128)} %reduce_sum.19), kind=kLoop, calls=%fused_computation.37 | loop fusion | flops 3712 | bytes 29696 | tf_op jit(solution)/shard_map/div | solution.py:102
  86.3 0.7 copy.134
  87.0 1.0 fusion.26
  88.3 0.7 copy.140
  89.1 1.6 %scatter_fusion = f32[32,58,128]{2,1,0:T(8,128)S(1)} fusion(f32[32,58,128]{2,1,0:T(8,128)S(1)} %max.12.clone, s32[32]{0:T(128)S(1)} %get-tuple-element.20, f32[32,58,128]{2,1,0:T(8,128)S(1)} %copy.137), kind=kCustom, calls=%fused_computation.2 | custom fusion | bytes 2850944 | tf_op jit(solution)/shard_map/scatter | solution.py:116
  90.7 18.5 %reduce-scatter.2.cloned.1.call-done = f32[32,116]{1,0:T(8,128)} async-done(((f32[128,116]{1,0:T(8,128)}), f32[32,116]{1,0:T(8,128)}) %reduce-scatter.2.cloned.1.call-update) | async-done | bytes 14864 | tf_op jit(solution)/shard_map/reduce_scatter | solution.py:176
  109.1 0.8 reshape.137
  109.9 0.6 copy.148
  110.5 0.8 scatter_fusion.1
  111.3 1.5 %copy.141 = f32[32,58,128]{2,0,1:T(8,128)} copy(f32[32,58,128]{2,1,0:T(8,128)S(1)} %scatter_fusion.1) | data formatting | bytes 1900544
  (51 shorter events, 2.7 us)
Async XLA Ops:
  7.2 15.3 %copy-start = (f32[32,58,128]{2,0,1:T(8,128)S(1)}, f32[32,58,128]{2,0,1:T(8,128)}, u32[]{:S(2)}) copy-start(f32[32,58,128]{2,0,1:T(8,128)} %param.11) | copy-start | bytes 2850820
  11.4 20.6 %collective-permute-start = (f32[117,1,32]{0,2,1:T(8,128)S(1)}, f32[117,1,32]{0,2,1:T(8,128)S(1)}, u32[]{:S(2)}, u32[]{:S(2)}) collective-permute-start(f32[117,1,32]{0,2,1:T(8,128)S(1)} %get-tuple-element.52), channel_id=1, source_target_pairs={{0,4},{4,8},{8,12},{12,16},{16,20},{20,24},{24,28},{28,0},{1,5},{5... | collective-permute-start | bytes 44936 | tf_op jit(solution)/shard_map/ppermute | solution.py:17
  11.9 20.1 %collective-permute-start.1 = (f32[117,1,32]{0,2,1:T(8,128)S(1)}, f32[117,1,32]{0,2,1:T(8,128)S(1)}, u32[]{:S(2)}, u32[]{:S(2)}) collective-permute-start(f32[117,1,32]{0,2,1:T(8,128)S(1)} %get-tuple-element.53), channel_id=1, source_target_pairs={{4,0},{8,4},{12,8},{16,12},{20,16},{24,20},{28,24},{0,28},{5,1},{9... | collective-permute-start | bytes 44936 | tf_op jit(solution)/shard_map/ppermute | solution.py:18
  18.9 12.9 %all-to-all-start = ((f32[8,1,1]{2,1,0:T(1,128)}), f32[8,1,1]{2,1,0:T(1,128)S(1)}, u32[]{:S(2)}, u32[]{:S(2)}) async-start(f32[8,1,1]{2,1,0:T(1,128)} %copy.138), calls=%async_computation.1 | async-start | bytes 8192 | tf_op jit(solution)/shard_map/all_to_all | solution.py:130
  30.2 1.6 %copy-start.3 = (s32[32]{0:T(128)S(1)}, s32[32]{0:T(128)}, u32[]{:S(2)}) copy-start(s32[32]{0:T(128)} %param.13) | copy-start | bytes 388
  30.2 22.2 %copy-start.2 = (s32[32]{0:T(128)S(1)}, s32[32]{0:T(128)}, u32[]{:S(2)}) copy-start(s32[32]{0:T(128)} %param.12) | copy-start | bytes 388
  32.1 5.8 %collective-permute-start.2 = (f32[117,6,1]{0,2,1:T(1,128)S(1)}, f32[117,6,1]{0,2,1:T(1,128)S(1)}, u32[]{:S(2)}, u32[]{:S(2)}) collective-permute-start(f32[117,6,1]{0,2,1:T(1,128)S(1)} %get-tuple-element.54), channel_id=1, source_target_pairs={{0,1},{1,2},{2,3},{3,0},{4,5},{5,6},{6,7},{7,4},{8,9},{9,10},{10,1... | collective-permute-start | bytes 8432 | tf_op jit(solution)/shard_map/ppermute | solution.py:17
  34.3 3.6 %collective-permute-start.3 = (f32[117,6,1]{0,2,1:T(1,128)S(1)}, f32[117,6,1]{0,2,1:T(1,128)S(1)}, u32[]{:S(2)}, u32[]{:S(2)}) collective-permute-start(f32[117,6,1]{0,2,1:T(1,128)S(1)} %get-tuple-element.55), channel_id=1, source_target_pairs={{1,0},{2,1},{3,2},{0,3},{5,4},{6,5},{7,6},{4,7},{9,8},{10,9},{11,1... | collective-permute-start | bytes 8432 | tf_op jit(solution)/shard_map/ppermute | solution.py:18
  75.3 35.2 %all-to-all-start.1 = ((f32[8,58,128]{2,1,0:T(8,128)}), f32[8,58,128]{2,1,0:T(8,128)S(1)}, u32[]{:S(2)}, u32[]{:S(2)}) async-start(f32[8,58,128]{2,1,0:T(8,128)} %broadcast_multiply_fusion), calls=%async_computation.2 | async-start | bytes 524288 | tf_op jit(solution)/shard_map/all_to_all | solution.py:129
  79.4 29.7 %reduce-scatter.2.cloned.1.call-start = ((), (), s32[]{:S(2)}) async-start(), calls=%async_computation.3 | async-start | bytes 81920 | tf_op jit(solution)/shard_map/reduce_scatter | solution.py:176
  85.0 3.0 %copy-start.1 = (f32[2,58,4,32]{1,3,2,0:T(8,128)S(1)}, f32[2,58,4,32]{1,3,2,0:T(8,128)}, u32[]{:S(2)}) copy-start(f32[2,58,4,32]{1,3,2,0:T(8,128)} %param.8) | copy-start | bytes 178180
Sparse Core Ops, SparseCore 0:
  88.1 20.9 reduce-scatter.1
where the time goes:
time: 120 us
  local copies, waits for them, and re-layouts  33.3 us (28%)
  other arithmetic  20.4 us (17%)
  waiting for transfers between devices  20 us (17%)
  starting transfers between devices  15.5 us (13%)
  between operations  14.3 us (12%)
  blocking collectives  13.6 us (11%)
  matrix products  2.52 us (2%)
    reduce_scatter x1, waiting for transfers between devices, on_device(): lax.psum_scatter(jnp.einsum('cs,ks->ck', column_picker, flat_tendency, pr...  18.5 us
    all_gather x1, blocking collectives, on_device(): partition_piece = lax.all_gather(forcing, 'mem', axis=2, tiled=True)  13.6 us
    sub x1, other arithmetic, crm_run(): change = current - state  6.12 us
    select_n x1, other arithmetic, crm_run(): current = jnp.where(active, updated, current)  5.14 us
    ppermute x2, starting transfers between devices, extended(): after = lax.ppermute(first, axis, down)  5.01 us
    all_to_all x1, starting transfers between devices, relocate(): lax.all_to_all(bucket_state, 'grp', split_axis=0, concat_axis=0, tiled=True)  4.08 us
    all_to_all x1, starting transfers between devices, relocate(): lax.all_to_all(holding_bucket_side, 'grp', split_axis=0, concat_axis=0, t...  3.52 us
    slice x2, local copies, waits for them, and re-layouts, crm_run(): jnp.roll(current, -1, -1)  3.24 us
  transfers between devices with their start and end apart: 7, of which 2 were waited for; matrix products, arithmetic and copies ran while one was open for 22% of the time, Pallas kernels for 0%

commit v1 on v0

v1 whole, which is shorter than its diff:
```python
import functools

import jax
import jax.numpy as jnp
import numpy as np
from jax import lax
from jax.experimental import pallas as pl
from jax.experimental.pallas import tpu as pltpu
from jax.sharding import PartitionSpec as P

NSUB = 2
MESH = pl.DeviceIdType.MESH
F32 = jnp.float32
BF16 = jnp.bfloat16
LANES = 128


def derivative_table():
    nodes = np.array([-1.0, -1.0 / np.sqrt(5.0), 1.0 / np.sqrt(5.0), 1.0])
    table = np.zeros((4, 4))
    for i in range(4):
        for j in range(4):
            if i == j:
                table[i, j] = sum(1.0 / (nodes[j] - nodes[o]) for o in range(4) if o != j)
            else:
                top, bottom = 1.0, 1.0
                for o in range(4):
                    if o != j and o != i:
                        top = top * (nodes[i] - nodes[o])
                    if o != j:
                        bottom = bottom * (nodes[j] - nodes[o])
                table[i, j] = top / bottom
    return table.astype(np.float32)


def split(values):
    high = values.astype(BF16)
    low = (values - high.astype(F32)).astype(BF16)
    return jnp.concatenate([high, low], axis=-1)


def explicit_part(cur, width):
    lane = lax.broadcasted_iota(jnp.int32, cur.shape, 1)
    heat = lane < width
    inner = lane % width
    other = pltpu.roll(cur, width, 1)
    diff = other - cur
    gap = jnp.where(heat, diff, -diff)
    condense = jnp.maximum(gap, 0.0) + jnp.log(1.0 + jnp.exp(-jnp.abs(gap)))
    left = jnp.where(inner == 0, pltpu.roll(cur, width + 1, 1), pltpu.roll(cur, 1, 1))
    right = jnp.where(
        inner == width - 1,
        pltpu.roll(cur, width - 1, 1),
        pltpu.roll(cur, 2 * width - 1, 1),
    )
    upper = jnp.concatenate([cur[1:], cur[-1:]], 0)
    lower = jnp.concatenate([cur[:1], cur[:-1]], 0)
    scale = jnp.where(heat, 0.05, -0.1)
    return 0.5 * cur + 0.15 * (left + right) + 0.1 * (upper + lower) + scale * condense


def exchange(n_grp, n_mem, levels, rows, points, slots, width, *refs):
    (dyn_ref, wind_ref, mass_ref, crm_hbm, bmap_ref, steps_ref, migrate_ref,
     deriv_ref, spread_ref, pick_ref,
     asm_ref, phys_ref, stepped_ref, arrived_ref,
     crm, part0, vt, vrow, edge_s, edge_x, edge_y_s, edge_y, edge_d_s, edge_d,
     pair, own_f, gathered, fslot, bucket, tend, outgoing, incoming,
     crm_sem, sx_sem, rx_sem, sy_sem, ry_sem, sd_sem, rd_sem,
     sg_sem, rg_sem, sb_sem, rb_sem, st_sem, rt_sem) = refs
    g, m = lax.axis_index("grp"), lax.axis_index("mem")
    fields = 2 * levels

    load = pltpu.make_async_copy(crm_hbm, crm, crm_sem)
    load.start()

    gu, gd = lax.rem(g + n_grp - 1, n_grp), lax.rem(g + 1, n_grp)
    ml, mr = lax.rem(m + n_mem - 1, n_mem), lax.rem(m + 1, n_mem)
    corners = ((gd, mr), (gd, ml), (gu, mr), (gu, ml))
    barrier = pltpu.get_barrier_semaphore()
    for o in range(1, n_grp):
        pl.semaphore_signal(barrier, 1, device_id=(lax.rem(g + o, n_grp), m), device_id_type=MESH)
    for o in range(1, n_mem):
        pl.semaphore_signal(barrier, 1, device_id=(g, lax.rem(m + o, n_mem)), device_id_type=MESH)
    for corner in corners:
        pl.semaphore_signal(barrier, 1, device_id=corner, device_id_type=MESH)

    deriv = deriv_ref[...]
    for r in range(rows):
        mass = mass_ref[r:r + 1, :]
        wind = wind_ref[pl.ds(r, levels, stride=rows), :]
        factor = -wind * mass
        for f in range(2):
            x = dyn_ref[pl.ds(f * levels * rows + r, levels, stride=rows), :]
            dx = jnp.dot(x, deriv, precision=lax.Precision.HIGHEST, preferred_element_type=F32)
            vrow[pl.ds(f * levels, levels), :] = factor * dx
        vrow[pl.ds(fields, LANES - fields), :] = jnp.broadcast_to(mass, (LANES - fields, points))
        value = vrow[...].T
        vt[r] = value
        edge_s[0, r:r + 1, :] = value[points - 1:, :]
        edge_s[1, r:r + 1, :] = value[:1, :]
        if r == rows - 1:
            edge_y_s[0] = value
            edge_d_s[0, 0:1, :] = value[points - 1:, :]
            edge_d_s[1, 0:1, :] = value[:1, :]
        if r == 0:
            edge_y_s[1] = value
            edge_d_s[2, 0:1, :] = value[points - 1:, :]
            edge_d_s[3, 0:1, :] = value[:1, :]

    pl.semaphore_wait(barrier, n_grp - 1 + n_mem - 1 + 4)

    def remote(src, dst, ssem, rsem, device):
        return pltpu.make_async_remote_copy(
            src_ref=src, dst_ref=dst, send_sem=ssem, recv_sem=rsem,
            device_id=device, device_id_type=MESH)

    halos = []
    for i, corner in enumerate(corners):
        halos.append(remote(edge_d_s.at[i], edge_d.at[i], sd_sem.at[i], rd_sem.at[i], corner))
    for i, near in enumerate((gd, gu)):
        halos.append(remote(edge_y_s.at[i], edge_y.at[i], sy_sem.at[i], ry_sem.at[i], (near, m)))
    for i, near in enumerate((mr, ml)):
        halos.append(remote(edge_s.at[i], edge_x.at[i], sx_sem.at[i], rx_sem.at[i], (g, near)))
    for copy in halos:
        copy.start()

    load.wait()

    def first(s, carry):
        part0[s] = explicit_part(crm[s], width)
        return carry

    lax.fori_loop(0, slots, first, 0, unroll=2)

    for copy in halos:
        copy.wait()

    position = lax.broadcasted_iota(jnp.int32, (points, LANES), 0)

    def sweep(value, before, after):
        lower = jnp.where(position == 0, before, pltpu.roll(value, 1, 0))
        upper = jnp.where(position == points - 1, after, pltpu.roll(value, points - 1, 0))
        return (value + jnp.where(position % 4 == 0, lower, 0.0)
                + jnp.where(position % 4 == 3, upper, 0.0))

    swept = [sweep(edge_y[0], edge_d[0, 0:1, :], edge_d[1, 0:1, :])]
    for r in range(rows):
        swept.append(sweep(vt[r], edge_x[0, r:r + 1, :], edge_x[1, r:r + 1, :]))
    swept.append(sweep(edge_y[1], edge_d[2, 0:1, :], edge_d[3, 0:1, :]))
    results = []
    for r in range(rows):
        total = swept[r + 1]
        if r % 4 == 0:
            total = total + swept[r]
        if r % 4 == 3:
            total = total + swept[r + 2]
        result = total / total[:, fields:fields + 1]
        asm_ref[r] = result
        results.append(result)
    half = points // 2
    for b in range(rows // 2):
        pair[...] = 0.25 * (results[2 * b] + results[2 * b + 1])
        own_f[pl.ds(b * half, half), :] = (
            pair[pl.ds(0, half, stride=2), :] + pair[pl.ds(1, half, stride=2), :])

    here = pl.ds(pl.multiple_of(m * slots, slots), slots)
    sends = [
        remote(own_f, gathered.at[o - 1], sg_sem.at[o - 1], rg_sem.at[o - 1],
               (g, lax.rem(m + o, n_mem)))
        for o in range(1, n_mem)]
    for copy in sends:
        copy.start()
    cols = lax.broadcasted_iota(jnp.int32, (slots, slots), 1)
    served = bmap_ref[...]

    def place(source):
        mine = (served == cols + source * slots).astype(BF16)
        return mine

    total = jnp.dot(place(m), split(own_f[...]), preferred_element_type=F32)
    for o in range(1, n_mem):
        sends[o - 1].wait()
        total = total + jnp.dot(place(lax.rem(m + n_mem - o, n_mem)), split(gathered[o - 1]),
                                preferred_element_type=F32)
    fslot[...] = total

    def second(index):
        row = fslot[pl.ds(index, 1), :]
        chosen = (pick_ref[...] * row).astype(BF16)
        forced = 0.25 * jnp.dot(chosen, spread_ref[:, :LANES], preferred_element_type=F32)[:levels]
        start = crm[index]
        count = steps_ref[index]
        cur = jnp.where(count > 0, part0[index] + forced, start)
        cur = jnp.where(count > 1, explicit_part(cur, width) + forced, cur)
        return cur, start

    span = n_mem * slots

    def leave(i, carry):
        target = lax.rem(g + i + 1, n_grp)
        low = target * span + m * slots
        index, mark = jnp.int32(0), jnp.int32(0)
        for s in range(slots):
            where_to = migrate_ref[s]
            hit = (where_to >= low) & (where_to < low + slots)
            index = jnp.where(hit, s, index)
            mark = jnp.where(hit, where_to - low + 1, mark)
        cur, _ = second(index)
        bucket[i, 0:levels, :] = cur
        bucket[i, levels:, :] = jnp.full((bucket.shape[1] - levels, LANES), mark.astype(F32))
        remote(bucket.at[i], arrived_ref.at[i], sb_sem.at[i], rb_sem.at[i], (target, m)).start()
        return carry

    lax.fori_loop(0, n_grp - 1, leave, 0)

    def stay(s, carry):
        cur, start = second(s)
        stepped_ref[s] = cur
        change = jnp.dot(split(cur - start), spread_ref[:, LANES:], preferred_element_type=F32)
        chosen = jnp.where(pick_ref[0:levels, 0:LANES] > 0.0, change, 0.0)
        tend[pl.ds(s, 1), :] = jnp.sum(chosen, 0, keepdims=True) * (1.0 / width)
        return carry

    lax.fori_loop(0, slots, stay, 0, unroll=2)

    def route(dest):
        mine = (served == cols + dest * slots).astype(F32)
        return lax.dot_general(mine, tend[...], (((0,), (0,)), ((), ())),
                               precision=lax.Precision.HIGHEST, preferred_element_type=F32)

    returns = []
    for o in range(1, n_mem):
        dest = lax.rem(m + o, n_mem)
        outgoing[o - 1] = route(dest)
        copy = remote(outgoing.at[o - 1], incoming.at[o - 1], st_sem.at[o - 1], rt_sem.at[o - 1],
                      (g, dest))
        copy.start()
        returns.append(copy)
    sums = route(m)
    for o in range(1, n_mem):
        returns[o - 1].wait()
        sums = sums + incoming[o - 1]
    phys_ref[...] = sums

    def finish(i, carry):
        target = lax.rem(g + i + 1, n_grp)
        remote(bucket.at[i], arrived_ref.at[i], sb_sem.at[i], rb_sem.at[i], (target, m)).wait()
        return carry

    lax.fori_loop(0, n_grp - 1, finish, 0)


def place_outputs(n_grp, n_mem, levels, rows, points, slots, *refs):
    (migrate_ref, dyn_ref, asm_ref, phys_ref, stepped_ref, arrived_ref,
     dyn_out, phys_out, crm_out) = refs
    g = lax.axis_index("grp")
    fields = 2 * levels
    span = n_mem * slots
    low = g * span
    for s in range(slots):
        where_to = migrate_ref[s]

        @pl.when((where_to >= low) & (where_to < low + span))
        def _():
            crm_out[lax.rem(where_to, slots)] = stepped_ref[s]

    for r in range(rows):
        back = asm_ref[r].T
        at = pl.ds(r, fields, stride=rows)
        dyn_out[at, :] = dyn_ref[at, :] + 0.2 * back[:fields]
    turned = phys_ref[...].T
    phys_out[0] = turned[:levels]
    phys_out[1] = turned[levels:fields]

    def settle(i, carry):
        mark = jnp.max(arrived_ref[i, levels:levels + 1, :]).astype(jnp.int32)

        @pl.when(mark > 0)
        def _():
            crm_out[mark - 1] = arrived_ref[i, 0:levels, :]

        return carry

    lax.fori_loop(0, n_grp - 1, settle, 0)


def on_device(n_grp, n_mem, dyn_state, wind_speed, mass_weight, crm_state, batch_map, sub_steps,
              migrate_to):
    _, levels, rows, points = dyn_state.shape
    slots = crm_state.shape[0]
    width = crm_state.shape[2] // 2
    fields = 2 * levels
    padded = levels // 8 * 8 + 8
    deriv = np.kron(np.eye(points // 4), derivative_table().T).astype(np.float32)
    k = np.arange(LANES)
    half_of_k = np.where(k < fields, k // levels, 2)
    half_of_x = np.arange(2 * width) // width
    same = (half_of_k[:, None] == half_of_x[None, :]).astype(np.float32)
    spread = np.concatenate([np.tile(same, (2, 1)), np.tile(same.T, (2, 1))], 1)
    pick = ((k[None, :] % levels == np.arange(padded)[:, None]) & (k[None, :] < fields))
    pick = np.tile(pick.astype(np.float32), (1, 2))
    dyn2 = dyn_state.reshape(fields * rows, points)
    wind2 = wind_speed.reshape(levels * rows, points)
    vmem = pl.BlockSpec(memory_space=pltpu.VMEM)
    smem = pl.BlockSpec(memory_space=pltpu.SMEM)
    hbm = pl.BlockSpec(memory_space=pl.ANY)
    dma = pltpu.SemaphoreType.DMA
    sds = jax.ShapeDtypeStruct
    asm, phys, stepped, arrived = pl.pallas_call(
        functools.partial(exchange, n_grp, n_mem, levels, rows, points, slots, width),
        out_shape=(
            sds((rows, points, LANES), F32),
            sds((slots, LANES), F32),
            sds((slots, levels, 2 * width), F32),
            sds((n_grp - 1, padded, LANES), F32),
        ),
        in_specs=[vmem, vmem, vmem, hbm, vmem, smem, smem, vmem, vmem, vmem],
        out_specs=(vmem, vmem, vmem, hbm),
        scratch_shapes=[
            pltpu.VMEM((slots, levels, 2 * width), F32),
            pltpu.VMEM((slots, levels, 2 * width), F32),
            pltpu.VMEM((rows, points, LANES), F32),
            pltpu.VMEM((LANES, points), F32),
            pltpu.VMEM((2, 8, LANES), F32),
            pltpu.VMEM((2, 8, LANES), F32),
            pltpu.VMEM((2, points, LANES), F32),
            pltpu.VMEM((2, points, LANES), F32),
            pltpu.VMEM((4, 8, LANES), F32),
            pltpu.VMEM((4, 8, LANES), F32),
            pltpu.VMEM((points, LANES), F32),
            pltpu.VMEM((slots, LANES), F32),
            pltpu.VMEM((n_mem - 1, slots, LANES), F32),
            pltpu.VMEM((slots, 2 * LANES), F32),
            pltpu.VMEM((n_grp - 1, padded, LANES), F32),
            pltpu.VMEM((slots, LANES), F32),
            pltpu.VMEM((n_mem - 1, slots, LANES), F32),
            pltpu.VMEM((n_mem - 1, slots, LANES), F32),
            dma,
            dma((2,)), dma((2,)), dma((2,)), dma((2,)), dma((4,)), dma((4,)),
            dma((n_mem - 1,)), dma((n_mem - 1,)),
            dma((n_grp - 1,)), dma((n_grp - 1,)),
            dma((n_mem - 1,)), dma((n_mem - 1,)),
        ],
        compiler_params=pltpu.CompilerParams(collective_id=0, has_side_effects=True),
        name="exchange",
    )(dyn2, wind2, mass_weight, crm_state, batch_map[:, None], sub_steps, migrate_to,
      jnp.asarray(deriv), jnp.asarray(spread).astype(BF16), jnp.asarray(pick))
    dyn_next, phys_tend, crm_next = pl.pallas_call(
        functools.partial(place_outputs, n_grp, n_mem, levels, rows, points, slots),
        out_shape=(
            sds((fields * rows, points), F32),
            sds((2, levels, slots), F32),
            sds((slots, levels, 2 * width), F32),
        ),
        in_specs=[smem, vmem, vmem, vmem, vmem, vmem],
        out_specs=(vmem, vmem, vmem),
        name="place",
    )(migrate_to, dyn2, asm, phys, stepped, arrived)
    return dyn_next.reshape(dyn_state.shape), phys_tend, crm_next


def solution(mesh):
    n_grp, n_mem = mesh.shape["grp"], mesh.shape["mem"]
    grid = P(None, None, "grp", "mem")
    slot = P(("grp", "mem"))
    return jax.shard_map(
        functools.partial(on_device, n_grp, n_mem),
        mesh=mesh,
        in_specs=(grid, P(None, "grp", "mem"), P("grp", "mem"), P(("grp", "mem"), None, None),
                  slot, slot, slot),
        out_specs=(grid, P(None, None, ("grp", "mem")), P(("grp", "mem"), None, None)),
        check_vma=False,
    )
```

time: 120 us -> 45.9 us (0.38)
  Pallas kernels: 0 us -> 33.2 us
  local copies, waits for them, and re-layouts: 33.3 us -> 11.7 us
  other arithmetic: 20.4 us -> 0 us
  waiting for transfers between devices: 20 us -> 0 us
  starting transfers between devices: 15.5 us -> 0 us
  between operations: 14.3 us -> 0.66 us
  blocking collectives: 13.6 us -> 0 us
  matrix products: 2.52 us -> 0 us
    pallas_call x0 -> x2, Pallas kernels: none -> 33.2 us  [the longest x1 29.3 us: on_device(): pl.pallas_call(functools.partial(exchange, n_grp, n_mem, levels, rows, po...]
    slice x16 -> x0, local copies, waits for them, and re-layouts: 18.6 us -> none  [the longest x2 3.24 us: crm_run(): jnp.roll(current, -1, -1)]
    reduce_scatter x1 -> x0, waiting for transfers between devices: 18.5 us -> none  [on_device(): lax.psum_scatter(jnp.einsum('cs,ks->ck', column_picker, flat_tendency, pr...]
    all_gather x1 -> x0, blocking collectives: 13.6 us -> none  [on_device(): partition_piece = lax.all_gather(forcing, 'mem', axis=2, tiled=True)]
    unnamed x10 -> x12, local copies, waits for them, and re-layouts: 2.17 us -> 11 us
    ppermute x4 -> x0, starting transfers between devices: 7.64 us -> none  [the longest x2 5.01 us: extended(): after = lax.ppermute(first, axis, down)]
    all_to_all x2 -> x0, starting transfers between devices: 7.6 us -> none  [the longest x1 4.08 us: relocate(): lax.all_to_all(bucket_state, 'grp', split_axis=0, concat_axis=0, tiled=True)]
    select_n x5 -> x0, other arithmetic: 6.48 us -> none  [the longest x1 5.14 us: crm_run(): current = jnp.where(active, updated, current)]
  transfers between devices with their start and end apart: 7 -> 0, of which waited for: 2 -> 0; matrix products, arithmetic and copies ran while one was open for 22% -> 0% of each run, Pallas kernels for 0% -> 0%
where the time goes in v1:
time: 45.9 us; the launch traced here: 45.6 us
  Pallas kernels  33.2 us (72%)
  local copies, waits for them, and re-layouts  11.7 us (25%)
  between operations  0.66 us (1%)
    pallas_call x1, Pallas kernels, on_device(): pl.pallas_call(functools.partial(exchange, n_grp, n_mem, levels, rows, po...  29.3 us
    unnamed x12, local copies, waits for them, and re-layouts  11 us
    pallas_call x1, Pallas kernels, on_device(): pl.pallas_call(functools.partial(place_outputs, n_grp, n_mem, levels, row...  3.93 us

profile of v1, /device:TPU:0, one launch (start us, length us, event | category | flops | bytes accessed | tf_op | source)
XLA Modules:
  0.0 45.6 jit_solution(17016018891355628050)
XLA Ops:
  0.6 0.0 copy-start.2
  0.6 0.0 copy-start
  0.6 0.6 %copy-done.2 = s32[32]{0:T(128)S(1)} copy-done((s32[32]{0:T(128)S(1)}, s32[32]{0:T(128)}, u32[]{:S(2)}) %copy-start.2) | copy-done | bytes 152
  1.3 0.7 %copy.16.refs_4_ = s32[32,1]{1,0:T(8,128)} copy(s32[32,1]{0,1:T(1,128)S(1)} %bitcast.8) | data formatting | bytes 256 | tf_op jit(solution)/shard_map/broadcast_in_dim | solution.py:346
  2.0 1.6 %copy.14 = f32[58,4,32]{2,1,0:T(4,128)} copy(f32[58,4,32]{0,2,1:T(8,128)} %param.11) | data formatting | bytes 59392 | tf_op args[1]
  3.6 0.0 copy-done
  3.6 0.8 %copy.13 = f32[2,58,4,32]{3,2,1,0:T(4,128)} copy(f32[2,58,4,32]{1,3,2,0:T(8,128)S(1)} %copy-done) | data formatting | bytes 118784 | tf_op args[0]
  4.4 2.8 %copy.15.refs_3_ = f32[32,58,128]{2,1,0:T(8,128)} copy(f32[32,58,128]{2,0,1:T(8,128)} %param.13) | data formatting | bytes 1900544 | tf_op args[3]
  7.2 29.3 %exchange.1 = (f32[4,32,128]{2,1,0:T(8,128)}, f32[32,128]{1,0:T(8,128)}, f32[32,58,128]{2,1,0:T(8,128)}, f32[7,64,128]{2,1,0:T(8,128)}) custom-call(f32[464,32]{1,0:T(8,128)} %bitcast.4, f32[232,32]{1,0:T(8,128)} %bitcast.6, f32[4,32]{1,0:T(4,128)} %refs_2_.1, f32[32,58,128]{2,1,0:T(8,128)} %copy.15.refs_3_, s32[32,1]{1,0:T(8,128)} %copy.16.refs_4_, ...), custom_call_target="tpu_custom_call" | custom-call | tf_op jit(solution)/shard_map/exchange/pallas_call | solution.py:309
  36.4 3.9 %place.1 = (f32[464,32]{1,0:T(8,128)}, f32[2,58,32]{2,1,0:T(8,128)}, f32[32,58,128]{2,1,0:T(8,128)}) custom-call(s32[32]{0:T(128)} %refs_0_.1, f32[464,32]{1,0:T(8,128)} %bitcast.5, f32[4,32,128]{2,1,0:T(8,128)} %get-tuple-element.10.refs_2_, f32[32,128]{1,0:T(8,128)} %get-tuple-element.11.refs_3_, f32[32,58,128]{2,1,0:T(8,128)} %get-tuple-element.12.refs_4_, ...), custom_call_target="tpu_custom_call" | custom-call | tf_op jit(solution)/shard_map/place/pallas_call | solution.py:348
  40.4 0.0 copy-start.1
  40.4 1.8 %copy.17 = f32[2,58,4,32]{1,3,2,0:T(8,128)} copy(f32[2,58,4,32]{3,2,1,0:T(4,128)} %bitcast.7) | data formatting | bytes 118784
  42.1 0.0 copy-done.1
  42.1 0.7 %copy.18 = f32[2,58,32]{1,2,0:T(8,128)} copy(f32[2,58,32]{2,1,0:T(8,128)S(1)} %copy-done.1) | data formatting | bytes 29696
  42.8 2.7 %copy.19 = f32[32,58,128]{2,0,1:T(8,128)} copy(f32[32,58,128]{2,1,0:T(8,128)} %get-tuple-element.19) | data formatting | bytes 1900544
Async XLA Ops:
  0.6 0.7 %copy-start.2 = (s32[32]{0:T(128)S(1)}, s32[32]{0:T(128)}, u32[]{:S(2)}) copy-start(s32[32]{0:T(128)} %param.14) | copy-start | bytes 388
  0.6 2.9 %copy-start = (f32[2,58,4,32]{1,3,2,0:T(8,128)S(1)}, f32[2,58,4,32]{1,3,2,0:T(8,128)}, u32[]{:S(2)}) copy-start(f32[2,58,4,32]{1,3,2,0:T(8,128)} %param.10) | copy-start | bytes 178180
  40.4 1.8 %copy-start.1 = (f32[2,58,32]{2,1,0:T(8,128)S(1)}, f32[2,58,32]{2,1,0:T(8,128)}, u32[]{:S(2)}) copy-start(f32[2,58,32]{2,1,0:T(8,128)} %get-tuple-element.18) | copy-start | bytes 44548

commit v2 on v1

v2 whole, which is shorter than its diff:
```python
import functools

import jax
import jax.numpy as jnp
import numpy as np
from jax import lax
from jax.experimental import pallas as pl
from jax.experimental.pallas import tpu as pltpu
from jax.sharding import PartitionSpec as P

NSUB = 2
MESH = pl.DeviceIdType.MESH
F32 = jnp.float32
BF16 = jnp.bfloat16
LANES = 128
UNROLL = 8


def derivative_table():
    nodes = np.array([-1.0, -1.0 / np.sqrt(5.0), 1.0 / np.sqrt(5.0), 1.0])
    table = np.zeros((4, 4))
    for i in range(4):
        for j in range(4):
            if i == j:
                table[i, j] = sum(1.0 / (nodes[j] - nodes[o]) for o in range(4) if o != j)
            else:
                top, bottom = 1.0, 1.0
                for o in range(4):
                    if o != j and o != i:
                        top = top * (nodes[i] - nodes[o])
                    if o != j:
                        bottom = bottom * (nodes[j] - nodes[o])
                table[i, j] = top / bottom
    return table.astype(np.float32)


def split(values):
    high = values.astype(BF16)
    low = (values - high.astype(F32)).astype(BF16)
    return jnp.concatenate([high, low], axis=-1)


def half_steps(cur, upper, lower, width):
    lane = lax.broadcasted_iota(jnp.int32, cur.shape, 1)
    heat = lane < width
    inner = lane % width
    other = pltpu.roll(cur, width, 1)
    diff = other - cur
    gap = jnp.where(heat, diff, -diff)
    condense = jnp.maximum(gap, 0.0) + jnp.log(1.0 + jnp.exp(-jnp.abs(gap)))
    left = jnp.where(inner == 0, pltpu.roll(cur, width + 1, 1), pltpu.roll(cur, 1, 1))
    right = jnp.where(
        inner == width - 1,
        pltpu.roll(cur, width - 1, 1),
        pltpu.roll(cur, 2 * width - 1, 1),
    )
    scale = jnp.where(heat, 0.05, -0.1)
    return 0.5 * cur + 0.15 * (left + right) + 0.1 * (upper + lower) + scale * condense


def blocks(levels, unroll, body, carry):
    full = levels // unroll
    if full:
        carry = lax.fori_loop(0, full, lambda i, c: body(i * unroll, unroll, c), carry)
    if levels % unroll:
        carry = body(full * unroll, levels % unroll, carry)
    return carry


def exchange(n_grp, n_mem, levels, rows, points, slots, width, *refs):
    (dyn_ref, wind_ref, mass_ref, crm_hbm, bmap_ref, steps_ref, migrate_ref,
     deriv_ref, same_ref,
     asm_ref, phys_ref, stepped_ref, arrived_ref,
     crm, part, mid, xs, ws, edge_s, edge_x, edge_y_s, edge_y, edge_d_s, edge_d,
     pair, own_f, gathered, bucket, tend, outgoing, incoming, index_s, mark_s,
     crm_sem, sx_sem, rx_sem, sy_sem, ry_sem, sd_sem, rd_sem,
     sg_sem, rg_sem, sb_sem, rb_sem, st_sem, rt_sem) = refs
    g, m = lax.axis_index("grp"), lax.axis_index("mem")
    fields = 2 * levels
    span = n_mem * slots

    load = pltpu.make_async_copy(crm_hbm, crm, crm_sem)
    load.start()

    gu, gd = lax.rem(g + n_grp - 1, n_grp), lax.rem(g + 1, n_grp)
    ml, mr = lax.rem(m + n_mem - 1, n_mem), lax.rem(m + 1, n_mem)
    corners = ((gd, mr), (gd, ml), (gu, mr), (gu, ml))
    barrier = pltpu.get_barrier_semaphore()
    for o in range(1, n_grp):
        pl.semaphore_signal(barrier, 1, device_id=(lax.rem(g + o, n_grp), m), device_id_type=MESH)
    for o in range(1, n_mem):
        pl.semaphore_signal(barrier, 1, device_id=(g, lax.rem(m + o, n_mem)), device_id_type=MESH)
    for corner in corners:
        pl.semaphore_signal(barrier, 1, device_id=corner, device_id_type=MESH)

    for r in range(rows):
        at = pl.ds(r * points, points)
        for f in range(2):
            xs[at, f * levels:(f + 1) * levels] = dyn_ref[f, r]
            ws[at, f * levels:(f + 1) * levels] = wind_ref[r]
        spread_mass = jnp.broadcast_to(mass_ref[r:r + 1, :], (LANES, points)).T
        xs[at, fields:] = jnp.zeros((points, LANES - fields), F32)
        ws[at, fields:] = -spread_mass[:, fields:]
    lane = lax.broadcasted_iota(jnp.int32, (points, LANES), 1)
    values = []
    dx = jnp.dot(deriv_ref[...], xs[...], precision=lax.Precision.HIGHEST,
                 preferred_element_type=F32)
    for r in range(rows):
        at = slice(r * points, (r + 1) * points)
        spread_mass = jnp.broadcast_to(mass_ref[r:r + 1, :], (LANES, points)).T
        advected = -ws[at] * jnp.where(lane < fields, dx[at] * spread_mass, 1.0)
        values.append(advected)
        edge_s[0, r:r + 1, :] = advected[points - 1:, :]
        edge_s[1, r:r + 1, :] = advected[:1, :]
        if r == rows - 1:
            edge_y_s[0] = advected
            edge_d_s[0, 0:1, :] = advected[points - 1:, :]
            edge_d_s[1, 0:1, :] = advected[:1, :]
        if r == 0:
            edge_y_s[1] = advected
            edge_d_s[2, 0:1, :] = advected[points - 1:, :]
            edge_d_s[3, 0:1, :] = advected[:1, :]

    pl.semaphore_wait(barrier, n_grp - 1 + n_mem - 1 + 4)

    def remote(src, dst, ssem, rsem, device):
        return pltpu.make_async_remote_copy(
            src_ref=src, dst_ref=dst, send_sem=ssem, recv_sem=rsem,
            device_id=device, device_id_type=MESH)

    halos = []
    for i, corner in enumerate(corners):
        halos.append(remote(edge_d_s.at[i], edge_d.at[i], sd_sem.at[i], rd_sem.at[i], corner))
    for i, near in enumerate((gd, gu)):
        halos.append(remote(edge_y_s.at[i], edge_y.at[i], sy_sem.at[i], ry_sem.at[i], (near, m)))
    for i, near in enumerate((mr, ml)):
        halos.append(remote(edge_s.at[i], edge_x.at[i], sx_sem.at[i], rx_sem.at[i], (g, near)))
    for copy in halos:
        copy.start()

    def find(i, carry):
        low = lax.rem(g + i + 1, n_grp) * span + m * slots
        index, mark = jnp.int32(0), jnp.int32(0)
        for s in range(slots):
            where_to = migrate_ref[s]
            hit = (where_to >= low) & (where_to < low + slots)
            index = jnp.where(hit, s, index)
            mark = jnp.where(hit, where_to - low + 1, mark)
        index_s[i] = index
        mark_s[i] = mark
        return carry

    lax.fori_loop(0, n_grp - 1, find, 0)

    load.wait()

    def slab(ref, level):
        start = level * slots
        if not isinstance(level, int):
            start = pl.multiple_of(start, slots)
        return ref[pl.ds(start, slots), :]

    def put(ref, level, value):
        start = level * slots
        if not isinstance(level, int):
            start = pl.multiple_of(start, slots)
        ref[pl.ds(start, slots), :] = value

    def clamp(level):
        if isinstance(level, int):
            return min(max(level, 0), levels - 1)
        return jnp.clip(level, 0, levels - 1)

    def explicit(ref, first, count):
        around = [slab(ref, clamp(first + j)) for j in range(-1, count + 1)]
        return [half_steps(around[j + 1], around[j + 2], around[j], width)
                for j in range(count)]

    def first_pass(first, count, carry):
        for j, value in enumerate(explicit(crm, first, count)):
            put(part, first + j, value)
        return carry

    blocks(levels, UNROLL, first_pass, 0)

    for copy in halos:
        copy.wait()

    position = lax.broadcasted_iota(jnp.int32, (points, LANES), 0)

    def sweep(value, before, after):
        lower = jnp.where(position == 0, before, pltpu.roll(value, 1, 0))
        upper = jnp.where(position == points - 1, after, pltpu.roll(value, points - 1, 0))
        return (value + jnp.where(position % 4 == 0, lower, 0.0)
                + jnp.where(position % 4 == 3, upper, 0.0))

    swept = [sweep(edge_y[0], edge_d[0, 0:1, :], edge_d[1, 0:1, :])]
    for r in range(rows):
        swept.append(sweep(values[r], edge_x[0, r:r + 1, :], edge_x[1, r:r + 1, :]))
    swept.append(sweep(edge_y[1], edge_d[2, 0:1, :], edge_d[3, 0:1, :]))
    results = []
    for r in range(rows):
        total = swept[r + 1]
        if r % 4 == 0:
            total = total + swept[r]
        if r % 4 == 3:
            total = total + swept[r + 2]
        result = total / total[:, fields:fields + 1]
        asm_ref[r] = result
        results.append(result)
    half = points // 2
    for b in range(rows // 2):
        pair[...] = 0.25 * (results[2 * b] + results[2 * b + 1])
        own_f[pl.ds(b * half, half), :] = (
            pair[pl.ds(0, half, stride=2), :] + pair[pl.ds(1, half, stride=2), :])

    sends = [
        remote(own_f, gathered.at[o - 1], sg_sem.at[o - 1], rg_sem.at[o - 1],
               (g, lax.rem(m + o, n_mem)))
        for o in range(1, n_mem)]
    for copy in sends:
        copy.start()
    column = lax.broadcasted_iota(jnp.int32, (slots, slots), 0)
    served = jnp.broadcast_to(bmap_ref[...], (slots, slots))

    def pick(source, rows_there):
        mine = (served == column + source * slots).astype(F32)
        return lax.dot_general(mine, rows_there, (((0,), (0,)), ((), ())),
                               precision=lax.Precision.HIGHEST, preferred_element_type=F32)

    count = jnp.broadcast_to(steps_ref[...].astype(F32), (LANES, slots)).T
    forcing = pick(m, own_f[...])
    for o in range(1, n_mem):
        sends[o - 1].wait()
        forcing = forcing + pick(lax.rem(m + n_mem - o, n_mem), gathered[o - 1])
    forcing = 0.25 * forcing

    lane_s = lax.broadcasted_iota(jnp.int32, (slots, LANES), 1)
    base = jnp.where(lane_s < width, 0, levels)

    def middle(first, number, carry):
        for j in range(number):
            force = jnp.take_along_axis(forcing, base + (first + j), axis=1)
            value = jnp.where(count > 0.5, slab(part, first + j) + force, slab(crm, first + j))
            put(mid, first + j, value)
            put(part, first + j, force)
        return carry

    blocks(levels, UNROLL, middle, 0)

    def leave(i, carry):
        target = lax.rem(g + i + 1, n_grp)
        at = pl.ds(index_s[i], levels, stride=slots)
        cur = mid[at, :]
        upper = jnp.concatenate([cur[1:], cur[-1:]], 0)
        lower = jnp.concatenate([cur[:1], cur[:-1]], 0)
        fresh = half_steps(cur, upper, lower, width) + part[at, :]
        twice = count_s[pl.ds(index_s[i], 1), :] > 1.5
        bucket[i, 0:levels, :] = jnp.where(twice, fresh, cur)
        bucket[i, levels:, :] = jnp.full((bucket.shape[1] - levels, LANES), mark_s[i].astype(F32))
        remote(bucket.at[i], arrived_ref.at[i], sb_sem.at[i], rb_sem.at[i], (target, m)).start()
        return carry

    count_s = tend
    count_s[...] = count
    if n_grp <= 8:
        for i in range(n_grp - 1):
            leave(i, 0)
    else:
        lax.fori_loop(0, n_grp - 1, leave, 0)

    def last(first, number, total):
        changes = []
        for j, fresh in enumerate(explicit(mid, first, number)):
            cur = jnp.where(count > 1.5, fresh + slab(part, first + j), slab(mid, first + j))
            put(stepped_ref, first + j, cur)
            changes.append(split(cur - slab(crm, first + j)))
        sums = jnp.dot(jnp.concatenate(changes, 0), same_ref[...], preferred_element_type=F32)
        for j in range(number):
            mine = lane_s - (first + j)
            mine = (mine == 0) | (mine == levels)
            total = jnp.where(mine, sums[j * slots:(j + 1) * slots], total)
        return total

    tendency = blocks(levels, UNROLL, last, jnp.zeros((slots, LANES), F32)) * (1.0 / width)

    def route(dest):
        mine = (served == column + dest * slots).astype(F32)
        return jnp.dot(mine, tendency, precision=lax.Precision.HIGHEST,
                       preferred_element_type=F32)

    returns = []
    for o in range(1, n_mem):
        dest = lax.rem(m + o, n_mem)
        outgoing[o - 1] = route(dest)
        copy = remote(outgoing.at[o - 1], incoming.at[o - 1], st_sem.at[o - 1], rt_sem.at[o - 1],
                      (g, dest))
        copy.start()
        returns.append(copy)
    sums = route(m)
    for o in range(1, n_mem):
        returns[o - 1].wait()
        sums = sums + incoming[o - 1]
    phys_ref[...] = sums

    def finish(i, carry):
        target = lax.rem(g + i + 1, n_grp)
        remote(bucket.at[i], arrived_ref.at[i], sb_sem.at[i], rb_sem.at[i], (target, m)).wait()
        return carry

    lax.fori_loop(0, n_grp - 1, finish, 0)


def place_outputs(n_grp, n_mem, levels, rows, points, slots, *refs):
    (migrate_ref, dyn_ref, asm_ref, phys_ref, stepped_ref, arrived_ref,
     dyn_out, phys_out, crm_out) = refs
    g = lax.axis_index("grp")
    span = n_mem * slots
    low = g * span
    for s in range(slots):
        where_to = migrate_ref[s]

        @pl.when((where_to >= low) & (where_to < low + span))
        def _():
            crm_out[pl.ds(lax.rem(where_to, slots), levels, stride=slots), :] = (
                stepped_ref[pl.ds(s, levels, stride=slots), :])

    for f in range(2):
        at = slice(f * levels, (f + 1) * levels)
        for r in range(rows):
            dyn_out[f, r] = dyn_ref[f, r] + 0.2 * asm_ref[r][:, at]
        phys_out[f] = phys_ref[...][:, at]

    def settle(i, carry):
        mark = jnp.max(arrived_ref[i, levels:levels + 1, :]).astype(jnp.int32)

        @pl.when(mark > 0)
        def _():
            crm_out[pl.ds(mark - 1, levels, stride=slots), :] = arrived_ref[i, 0:levels, :]

        return carry

    lax.fori_loop(0, n_grp - 1, settle, 0)


def on_device(n_grp, n_mem, dyn_state, wind_speed, mass_weight, crm_state, batch_map, sub_steps,
              migrate_to):
    _, levels, rows, points = dyn_state.shape
    slots = crm_state.shape[0]
    width = crm_state.shape[2] // 2
    fields = 2 * levels
    padded = levels // 8 * 8 + 8
    deriv = np.kron(np.eye(rows * points // 4), derivative_table()).astype(np.float32)
    k = np.arange(LANES)
    half_of_k = np.where(k < fields, k // levels, 2)
    half_of_x = np.arange(2 * width) // width
    same = np.tile((half_of_x[:, None] == half_of_k[None, :]).astype(np.float32), (2, 1))
    dyn2 = dyn_state.transpose(0, 2, 3, 1)
    wind2 = wind_speed.transpose(1, 2, 0)
    crm2 = crm_state.transpose(1, 0, 2).reshape(levels * slots, 2 * width)
    vmem = pl.BlockSpec(memory_space=pltpu.VMEM)
    smem = pl.BlockSpec(memory_space=pltpu.SMEM)
    hbm = pl.BlockSpec(memory_space=pl.ANY)
    dma = pltpu.SemaphoreType.DMA
    sds = jax.ShapeDtypeStruct
    buf = pltpu.VMEM
    asm, phys, stepped, arrived = pl.pallas_call(
        functools.partial(exchange, n_grp, n_mem, levels, rows, points, slots, width),
        out_shape=(
            sds((rows, points, LANES), F32),
            sds((slots, LANES), F32),
            sds((levels * slots, 2 * width), F32),
            sds((n_grp - 1, padded, LANES), F32),
        ),
        in_specs=[vmem, vmem, vmem, hbm, vmem, vmem, smem, vmem, vmem],
        out_specs=(vmem, vmem, vmem, hbm),
        scratch_shapes=[
            buf((levels * slots, 2 * width), F32),
            buf((levels * slots, 2 * width), F32),
            buf((levels * slots, 2 * width), F32),
            buf((rows * points, LANES), F32),
            buf((rows * points, LANES), F32),
            buf((2, 8, LANES), F32),
            buf((2, 8, LANES), F32),
            buf((2, points, LANES), F32),
            buf((2, points, LANES), F32),
            buf((4, 8, LANES), F32),
            buf((4, 8, LANES), F32),
            buf((points, LANES), F32),
            buf((slots, LANES), F32),
            buf((n_mem - 1, slots, LANES), F32),
            buf((n_grp - 1, padded, LANES), F32),
            buf((slots, LANES), F32),
            buf((n_mem - 1, slots, LANES), F32),
            buf((n_mem - 1, slots, LANES), F32),
            pltpu.SMEM((n_grp,), jnp.int32),
            pltpu.SMEM((n_grp,), jnp.int32),
            dma,
            dma((2,)), dma((2,)), dma((2,)), dma((2,)), dma((4,)), dma((4,)),
            dma((n_mem - 1,)), dma((n_mem - 1,)),
            dma((n_grp - 1,)), dma((n_grp - 1,)),
            dma((n_mem - 1,)), dma((n_mem - 1,)),
        ],
        compiler_params=pltpu.CompilerParams(collective_id=0, has_side_effects=True),
        name="exchange",
    )(dyn2, wind2, mass_weight, crm2, batch_map[None, :], sub_steps[None, :], migrate_to,
      jnp.asarray(deriv), jnp.asarray(same).astype(BF16))
    dyn_next, phys_tend, crm_next = pl.pallas_call(
        functools.partial(place_outputs, n_grp, n_mem, levels, rows, points, slots),
        out_shape=(
            sds(dyn2.shape, F32),
            sds((2, slots, levels), F32),
            sds((levels * slots, 2 * width), F32),
        ),
        in_specs=[smem, vmem, vmem, vmem, vmem, vmem],
        out_specs=(vmem, vmem, vmem),
        name="place",
    )(migrate_to, dyn2, asm, phys, stepped, arrived)
    crm_next = crm_next.reshape(levels, slots, 2 * width).transpose(1, 0, 2)
    return dyn_next.transpose(0, 3, 1, 2), phys_tend.transpose(0, 2, 1), crm_next


def solution(mesh):
    n_grp, n_mem = mesh.shape["grp"], mesh.shape["mem"]
    grid = P(None, None, "grp", "mem")
    slot = P(("grp", "mem"))
    return jax.shard_map(
        functools.partial(on_device, n_grp, n_mem),
        mesh=mesh,
        in_specs=(grid, P(None, "grp", "mem"), P("grp", "mem"), P(("grp", "mem"), None, None),
                  slot, slot, slot),
        out_specs=(grid, P(None, None, ("grp", "mem")), P(("grp", "mem"), None, None)),
        check_vma=False,
    )
```

time: 45.9 us -> 30.2 us (0.66)
  local copies, waits for them, and re-layouts: 11.7 us -> 0 us
  Pallas kernels: 33.2 us -> 29.4 us
    unnamed x12 -> x0, local copies, waits for them, and re-layouts: 11 us -> none
    pallas_call x1, Pallas kernels: 29.3 us -> 24.8 us  [on_device(): pl.pallas_call(functools.partial(exchange, n_grp, n_mem, levels, rows, po...]
    broadcast_in_dim x1 -> x0, local copies, waits for them, and re-layouts: 0.69 us -> none  [on_device(): batch_map[:, None]]
    pallas_call x1, Pallas kernels: 3.93 us -> 4.58 us  [on_device(): pl.pallas_call(functools.partial(place_outputs, n_grp, n_mem, levels, row...]
where the time goes in v2:
time: 30.2 us; the launch traced here: 30.1 us
  Pallas kernels  29.4 us (97%)
  between operations  0.64 us (2%)
    pallas_call x1, Pallas kernels, on_device(): pl.pallas_call(functools.partial(exchange, n_grp, n_mem, levels, rows, po...  24.8 us
    pallas_call x1, Pallas kernels, on_device(): pl.pallas_call(functools.partial(place_outputs, n_grp, n_mem, levels, row...  4.58 us

profile of v2, /device:TPU:0, one launch (start us, length us, event | category | flops | bytes accessed | tf_op | source)
XLA Modules:
  0.0 30.1 jit_solution(7695354675887313280)
XLA Ops:
  0.6 24.8 %exchange.1 = (f32[4,32,128]{2,1,0:T(8,128)}, f32[32,128]{1,0:T(8,128)}, f32[1856,128]{1,0:T(8,128)}, f32[7,64,128]{2,1,0:T(8,128)}) custom-call(f32[2,4,32,58]{3,2,1,0:T(8,128)} %bitcast.13, f32[4,32,58]{2,1,0:T(8,128)} %bitcast.15, f32[4,32]{1,0:T(4,128)} %refs_2_.1, f32[1856,128]{1,0:T(8,128)} %bitcast.12, s32[1,32]{1,0:T(1,128)} %bitcast.16, ...), custom_call_target="tpu_custom_call" | custom-call | tf_op jit(solution)/shard_map/exchange/pallas_call | solution.py:367
  25.5 4.6 %place.1 = (f32[2,4,32,58]{3,2,1,0:T(8,128)}, f32[2,32,58]{2,1,0:T(8,128)}, f32[1856,128]{1,0:T(8,128)}) custom-call(s32[32]{0:T(128)} %refs_0_.1, f32[2,4,32,58]{3,2,1,0:T(8,128)} %bitcast.14, f32[4,32,128]{2,1,0:T(8,128)} %get-tuple-element.10.refs_2_, f32[32,128]{1,0:T(8,128)} %get-tuple-element.11.refs_3_, f32[1856,128]{1,0:T(8,128)} %get-tuple-element.12.refs_4_, ...), custom_call_target="tpu_custom_call" | custom-call | tf_op jit(solution)/shard_map/place/pallas_call | solution.py:408

commit v3 on v2

--- a/solution.py
+++ b/solution.py
@@ -14,6 +14,7 @@
 BF16 = jnp.bfloat16
 LANES = 128
 UNROLL = 8
+CHUNK = 16
 
 
 def derivative_table():
@@ -68,19 +69,17 @@
 
 
 def exchange(n_grp, n_mem, levels, rows, points, slots, width, *refs):
-    (dyn_ref, wind_ref, mass_ref, crm_hbm, bmap_ref, steps_ref, migrate_ref,
-     deriv_ref, same_ref,
-     asm_ref, phys_ref, stepped_ref, arrived_ref,
+    (dyn_hbm, wind_hbm, mass_hbm, crm_hbm, bmap_hbm, steps_hbm, migrate_hbm,
+     deriv_hbm, same_hbm,
+     asm_hbm, phys_ref, stepped_hbm, arrived_ref,
+     dyn_ref, wind_ref, mass_ref, bmap_ref, steps_ref, migrate_ref, deriv_ref, same_ref, asm_ref,
      crm, part, mid, xs, ws, edge_s, edge_x, edge_y_s, edge_y, edge_d_s, edge_d,
      pair, own_f, gathered, bucket, tend, outgoing, incoming, index_s, mark_s,
-     crm_sem, sx_sem, rx_sem, sy_sem, ry_sem, sd_sem, rd_sem,
+     crm_sem, in_sem, asm_sem, out_sem, sx_sem, rx_sem, sy_sem, ry_sem, sd_sem, rd_sem,
      sg_sem, rg_sem, sb_sem, rb_sem, st_sem, rt_sem) = refs
     g, m = lax.axis_index("grp"), lax.axis_index("mem")
     fields = 2 * levels
     span = n_mem * slots
-
-    load = pltpu.make_async_copy(crm_hbm, crm, crm_sem)
-    load.start()
 
     gu, gd = lax.rem(g + n_grp - 1, n_grp), lax.rem(g + 1, n_grp)
     ml, mr = lax.rem(m + n_mem - 1, n_mem), lax.rem(m + 1, n_mem)
@@ -92,6 +91,17 @@
         pl.semaphore_signal(barrier, 1, device_id=(g, lax.rem(m + o, n_mem)), device_id_type=MESH)
     for corner in corners:
         pl.semaphore_signal(barrier, 1, device_id=corner, device_id_type=MESH)
+
+    pairs = ((dyn_hbm, dyn_ref), (deriv_hbm, deriv_ref), (wind_hbm, wind_ref),
+             (mass_hbm, mass_ref), (migrate_hbm, migrate_ref), (bmap_hbm, bmap_ref),
+             (steps_hbm, steps_ref), (same_hbm, same_ref))
+    loads = [pltpu.make_async_copy(a, b, in_sem.at[i]) for i, (a, b) in enumerate(pairs)]
+    for copy in loads:
+        copy.start()
+    load = pltpu.make_async_copy(crm_hbm, crm, crm_sem)
+    load.start()
+    for copy in loads:
+        copy.wait()
 
     for r in range(rows):
         at = pl.ds(r * points, points)
@@ -154,17 +164,20 @@
 
     load.wait()
 
+    stride = slots + 8
+
+    def rows_of(ref, level):
+        step = slots if ref is crm else stride
+        start = level * step
+        if not isinstance(level, int):
+            start = pl.multiple_of(start, 8)
+        return pl.ds(start, slots)
+
     def slab(ref, level):
-        start = level * slots
-        if not isinstance(level, int):
-            start = pl.multiple_of(start, slots)
-        return ref[pl.ds(start, slots), :]
+        return ref[rows_of(ref, level), :]
 
     def put(ref, level, value):
-        start = level * slots
-        if not isinstance(level, int):
-            start = pl.multiple_of(start, slots)
-        ref[pl.ds(start, slots), :] = value
+        ref[rows_of(ref, level), :] = value
 
     def clamp(level):
         if isinstance(level, int):
@@ -208,6 +221,7 @@
         result = total / total[:, fields:fields + 1]
         asm_ref[r] = result
         results.append(result)
+    asm_copy = pltpu.make_async_copy(asm_ref, asm_hbm, asm_sem)
     half = points // 2
     for b in range(rows // 2):
         pair[...] = 0.25 * (results[2 * b] + results[2 * b + 1])
@@ -220,20 +234,18 @@
         for o in range(1, n_mem)]
     for copy in sends:
         copy.start()
+    asm_copy.start()
     column = lax.broadcasted_iota(jnp.int32, (slots, slots), 0)
     served = jnp.broadcast_to(bmap_ref[...], (slots, slots))
 
-    def pick(source, rows_there):
-        mine = (served == column + source * slots).astype(F32)
-        return lax.dot_general(mine, rows_there, (((0,), (0,)), ((), ())),
-                               precision=lax.Precision.HIGHEST, preferred_element_type=F32)
-
+    origins = [m] + [lax.rem(m + n_mem - o, n_mem) for o in range(1, n_mem)]
+    mine = jnp.concatenate([served == column + at * slots for at in origins], 0).astype(F32).T
     count = jnp.broadcast_to(steps_ref[...].astype(F32), (LANES, slots)).T
-    forcing = pick(m, own_f[...])
-    for o in range(1, n_mem):
-        sends[o - 1].wait()
-        forcing = forcing + pick(lax.rem(m + n_mem - o, n_mem), gathered[o - 1])
-    forcing = 0.25 * forcing
+    for copy in sends:
+        copy.wait()
+    everyone = jnp.concatenate([own_f[...]] + [gathered[o] for o in range(n_mem - 1)], 0)
+    forcing = 0.25 * jnp.dot(mine, everyone, precision=lax.Precision.HIGHEST,
+                             preferred_element_type=F32)
 
     lane_s = lax.broadcasted_iota(jnp.int32, (slots, LANES), 1)
     base = jnp.where(lane_s < width, 0, levels)
@@ -250,7 +262,7 @@
 
     def leave(i, carry):
         target = lax.rem(g + i + 1, n_grp)
-        at = pl.ds(index_s[i], levels, stride=slots)
+        at = pl.ds(index_s[i], levels, stride=stride)
         cur = mid[at, :]
         upper = jnp.concatenate([cur[1:], cur[-1:]], 0)
         lower = jnp.concatenate([cur[:1], cur[:-1]], 0)
@@ -269,12 +281,20 @@
     else:
         lax.fori_loop(0, n_grp - 1, leave, 0)
 
+    def drain(first, number):
+        start = first * slots
+        if not isinstance(first, int):
+            start = pl.multiple_of(start, slots)
+        at = pl.ds(start, number * slots)
+        return pltpu.make_async_copy(crm.at[at], stepped_hbm.at[at], out_sem.at[first // UNROLL])
+
     def last(first, number, total):
         changes = []
         for j, fresh in enumerate(explicit(mid, first, number)):
             cur = jnp.where(count > 1.5, fresh + slab(part, first + j), slab(mid, first + j))
-            put(stepped_ref, first + j, cur)
             changes.append(split(cur - slab(crm, first + j)))
+            put(crm, first + j, cur)
+        drain(first, number).start()
         sums = jnp.dot(jnp.concatenate(changes, 0), same_ref[...], preferred_element_type=F32)
         for j in range(number):
             mine = lane_s - (first + j)
@@ -303,6 +323,13 @@
         sums = sums + incoming[o - 1]
     phys_ref[...] = sums
 
+    def drained(first, number, carry):
+        drain(first, number).wait()
+        return carry
+
+    blocks(levels, UNROLL, drained, 0)
+    asm_copy.wait()
+
     def finish(i, carry):
         target = lax.rem(g + i + 1, n_grp)
         remote(bucket.at[i], arrived_ref.at[i], sb_sem.at[i], rb_sem.at[i], (target, m)).wait()
@@ -312,35 +339,63 @@
 
 
 def place_outputs(n_grp, n_mem, levels, rows, points, slots, *refs):
-    (migrate_ref, dyn_ref, asm_ref, phys_ref, stepped_ref, arrived_ref,
-     dyn_out, phys_out, crm_out) = refs
+    (migrate_ref, dyn_ref, asm_ref, phys_ref, stepped_hbm, arrived_ref,
+     dyn_out, phys_out, crm_hbm, pool, placed, in_sem, out_sem) = refs
     g = lax.axis_index("grp")
     span = n_mem * slots
     low = g * span
-    for s in range(slots):
-        where_to = migrate_ref[s]
-
-        @pl.when((where_to >= low) & (where_to < low + span))
-        def _():
-            crm_out[pl.ds(lax.rem(where_to, slots), levels, stride=slots), :] = (
-                stepped_ref[pl.ds(s, levels, stride=slots), :])
-
+    stride = slots + 8
+    chunks = [(c, min(CHUNK, levels - c)) for c in range(0, levels, CHUNK)]
+    loads, stores = [], []
+    for i, (start, size) in enumerate(chunks):
+        levels_at, slots_at = pl.ds(start, size), pl.ds(0, slots)
+        loads.append(pltpu.make_async_copy(
+            stepped_hbm.at[levels_at], pool.at[levels_at, slots_at], in_sem.at[i]))
+        stores.append(pltpu.make_async_copy(
+            placed.at[levels_at, slots_at], crm_hbm.at[levels_at], out_sem.at[i]))
+    for copy in loads:
+        copy.start()
     for f in range(2):
         at = slice(f * levels, (f + 1) * levels)
         for r in range(rows):
             dyn_out[f, r] = dyn_ref[f, r] + 0.2 * asm_ref[r][:, at]
         phys_out[f] = phys_ref[...][:, at]
-
-    def settle(i, carry):
+    targets = []
+    for s in range(slots):
+        where_to = migrate_ref[s]
+        staying = (where_to >= low) & (where_to < low + span)
+        targets.append(jnp.where(staying, lax.rem(where_to, slots), slots))
+    flat_pool = pool.reshape(levels * stride, pool.shape[2])
+    flat_placed = placed.reshape(levels * stride, pool.shape[2])
+
+    def landing(i):
         mark = jnp.max(arrived_ref[i, levels:levels + 1, :]).astype(jnp.int32)
-
-        @pl.when(mark > 0)
-        def _():
-            crm_out[pl.ds(mark - 1, levels, stride=slots), :] = arrived_ref[i, 0:levels, :]
-
-        return carry
-
-    lax.fori_loop(0, n_grp - 1, settle, 0)
+        return jnp.where(mark > 0, mark - 1, slots)
+
+    few = n_grp <= 8
+    if few:
+        landings = [landing(i) for i in range(n_grp - 1)]
+    for i, (start, size) in enumerate(chunks):
+        loads[i].wait()
+        first = start * stride
+        for s in range(slots):
+            flat_placed[pl.ds(first + targets[s], size, stride=stride), :] = (
+                flat_pool[pl.ds(first + s, size, stride=stride), :])
+
+        def settle(j, carry):
+            target = landings[j] if few else landing(j)
+            flat_placed[pl.ds(first + target, size, stride=stride), :] = (
+                arrived_ref[j, start:start + size, :])
+            return carry
+
+        if few:
+            for j in range(n_grp - 1):
+                settle(j, 0)
+        else:
+            lax.fori_loop(0, n_grp - 1, settle, 0)
+        stores[i].start()
+    for copy in stores:
+        copy.wait()
 
 
 def on_device(n_grp, n_mem, dyn_state, wind_speed, mass_weight, crm_state, batch_map, sub_steps,
@@ -372,12 +427,21 @@
             sds((levels * slots, 2 * width), F32),
             sds((n_grp - 1, padded, LANES), F32),
         ),
-        in_specs=[vmem, vmem, vmem, hbm, vmem, vmem, smem, vmem, vmem],
-        out_specs=(vmem, vmem, vmem, hbm),
+        in_specs=[hbm] * 9,
+        out_specs=(hbm, vmem, hbm, hbm),
         scratch_shapes=[
+            buf(dyn2.shape, F32),
+            buf(wind2.shape, F32),
+            buf((rows, points), F32),
+            buf((1, slots), jnp.int32),
+            buf((1, slots), jnp.int32),
+            pltpu.SMEM((slots,), jnp.int32),
+            buf(deriv.shape, F32),
+            buf(same.shape, BF16),
+            buf((rows, points, LANES), F32),
             buf((levels * slots, 2 * width), F32),
-            buf((levels * slots, 2 * width), F32),
-            buf((levels * slots, 2 * width), F32),
+            buf((levels * (slots + 8), 2 * width), F32),
+            buf((levels * (slots + 8), 2 * width), F32),
             buf((rows * points, LANES), F32),
             buf((rows * points, LANES), F32),
             buf((2, 8, LANES), F32),
@@ -395,7 +459,7 @@
             buf((n_mem - 1, slots, LANES), F32),
             pltpu.SMEM((n_grp,), jnp.int32),
             pltpu.SMEM((n_grp,), jnp.int32),
-            dma,
+            dma, dma((8,)), dma, dma((levels // UNROLL + 1,)),
             dma((2,)), dma((2,)), dma((2,)), dma((2,)), dma((4,)), dma((4,)),
             dma((n_mem - 1,)), dma((n_mem - 1,)),
             dma((n_grp - 1,)), dma((n_grp - 1,)),
@@ -410,13 +474,18 @@
         out_shape=(
             sds(dyn2.shape, F32),
             sds((2, slots, levels), F32),
-            sds((levels * slots, 2 * width), F32),
+            sds((levels, slots, 2 * width), F32),
         ),
-        in_specs=[smem, vmem, vmem, vmem, vmem, vmem],
-        out_specs=(vmem, vmem, vmem),
+        in_specs=[smem, vmem, vmem, vmem, hbm, vmem],
+        out_specs=(vmem, vmem, hbm),
+        scratch_shapes=[
+            buf((levels, slots + 8, 2 * width), F32),
+            buf((levels, slots + 8, 2 * width), F32),
+            dma((levels // CHUNK + 1,)), dma((levels // CHUNK + 1,)),
+        ],
         name="place",
-    )(migrate_to, dyn2, asm, phys, stepped, arrived)
-    crm_next = crm_next.reshape(levels, slots, 2 * width).transpose(1, 0, 2)
+    )(migrate_to, dyn2, asm, phys, stepped.reshape(levels, slots, 2 * width), arrived)
+    crm_next = crm_next.transpose(1, 0, 2)
     return dyn_next.transpose(0, 3, 1, 2), phys_tend.transpose(0, 2, 1), crm_next
 
 

time: 30.2 us -> 28.2 us (0.934)
  Pallas kernels: 29.4 us -> 27.4 us
    pallas_call x1, Pallas kernels: 24.8 us -> 23.5 us  [on_device(): pl.pallas_call(functools.partial(exchange, n_grp, n_mem, levels, rows, po...]
    pallas_call x1, Pallas kernels: 4.58 us -> 3.86 us  [on_device(): pl.pallas_call(functools.partial(place_outputs, n_grp, n_mem, levels, row...]
where the time goes in v3:
time: 28.2 us; the launch traced here: 28 us
  Pallas kernels  27.4 us (97%)
  between operations  0.64 us (2%)
    pallas_call x1, Pallas kernels, on_device(): pl.pallas_call(functools.partial(exchange, n_grp, n_mem, levels, rows, po...  23.5 us
    pallas_call x1, Pallas kernels, on_device(): pl.pallas_call(functools.partial(place_outputs, n_grp, n_mem, levels, row...  3.86 us

profile of v3, /device:TPU:0, one launch (start us, length us, event | category | flops | bytes accessed | tf_op | source)
XLA Modules:
  0.0 28.0 jit_solution(3892690207443402714)
XLA Ops:
  0.6 23.5 %exchange.1 = (f32[4,32,128]{2,1,0:T(8,128)}, f32[32,128]{1,0:T(8,128)}, f32[1856,128]{1,0:T(8,128)}, f32[7,64,128]{2,1,0:T(8,128)}) custom-call(f32[2,4,32,58]{3,2,1,0:T(8,128)} %bitcast.13, f32[4,32,58]{2,1,0:T(8,128)} %bitcast.15, f32[4,32]{1,0:T(4,128)} %refs_2_.1, f32[1856,128]{1,0:T(8,128)} %bitcast.12, s32[1,32]{1,0:T(1,128)} %bitcast.16, ...), custom_call_target="tpu_custom_call" | custom-call | tf_op jit(solution)/shard_map/exchange/pallas_call | solution.py:422
  24.1 3.9 %place.1 = (f32[2,4,32,58]{3,2,1,0:T(8,128)}, f32[2,32,58]{2,1,0:T(8,128)}, f32[58,32,128]{2,1,0:T(8,128)}) custom-call(s32[32]{0:T(128)} %refs_0_.1, f32[2,4,32,58]{3,2,1,0:T(8,128)} %bitcast.14, f32[4,32,128]{2,1,0:T(8,128)} %get-tuple-element.10.refs_2_, f32[32,128]{1,0:T(8,128)} %get-tuple-element.11.refs_3_, f32[58,32,128]{2,1,0:T(8,128)} %bitcast.11, ...), custom_call_target="tpu_custom_call" | custom-call | tf_op jit(solution)/shard_map/place/pallas_call | solution.py:472
